TPU v7x, 32 devices: a whole 2x2x4 slice. The times are simulated.
32 devices in a mesh: tm: 2 (over x), member: 4 (over y, core), state: 4 (over z).
Axes of the slice: x: 2, y: 2, z: 4, core: 2. Of those that a mesh axis runs over, the one named last changes fastest.
Arguments:
- members: bfloat16 [4, 8, 16, 192, 1536], P('tm', 'member', None, 'state'), may hold values from -6 to 6
- slot_grad: float32 [4, 16, 192, 1536], P('tm', None, 'state'), may hold values from -6 to 6
- diffusivity: float32 [192, 1536], P('state'), may hold values from 0.03 to 0.24
- vertical: float32 [16, 16], replicated, may hold values from -0.3 to 2.1, as said below
Outputs:
- control_gradient: float32 [16, 8, 192, 1536], P('tm', 'member', 'state')
Inputs may be any that keep to these rules, and one draw needn't show every extreme that they name: `vertical`: the diagonal entries lie between 0.5 and 2.1.
All inputs are finite; a program needn't handle non-finite values.
Results may differ from a plain program's by a relative error of at most 0.0003.
Values sent between devices are 32-bit elements; how exact they have to be, the bound alone decides.
A program may use at most 128 MiB of HBM per device.

v0:
```python
import jax
import jax.numpy as jnp
from jax import lax
from jax.sharding import PartitionSpec as P

NSTEP = 4


def extended(x, sides, width):
    for axis, dim in sides:
        size, length = (lax.axis_size(axis), x.shape[dim])
        up = [(i, (i + 1) % size) for i in range(size - 1)]
        down = [(j, i) for i, j in up]
        last = lax.slice_in_dim(x, length - width, length, axis=dim)
        leading = lax.slice_in_dim(x, 0, width, axis=dim)
        before = lax.ppermute(last, axis, up)
        after = lax.ppermute(leading, axis, down)
        x = jnp.concatenate([before, x, after], axis=dim)
    return x


def stencil_update(centre, spread):
    middle = spread[..., 1:-1, :]
    return (
        centre
        + spread[..., 2:, :]
        + spread[..., :-2, :]
        + jnp.roll(middle, 1, -1)
        + jnp.roll(middle, -1, -1)
        - 4.0 * middle
    )


def body(members, slot_grad, diffusivity, vertical):
    ensemble = members.shape[1] * lax.axis_size("member")
    spread_scale = float(ensemble - 1) ** (-0.5)
    levels = members.shape[2]
    local_levels = levels // lax.axis_size("tm")
    partial_value = jnp.einsum(
        "smlrc,slrc->lmrc", members.astype(jnp.float32), slot_grad, precision=lax.Precision.HIGHEST
    )
    flattened = partial_value.reshape(levels, -1)
    product = jnp.dot(
        vertical.T, flattened, precision=lax.Precision.HIGHEST, preferred_element_type=jnp.float32
    )
    mixed_rows = lax.psum_scatter(
        product.reshape((lax.axis_size("tm") * local_levels,) + partial_value.shape[1:]),
        "tm",
        scatter_dimension=0,
        tiled=True,
    )
    product_sum = lax.psum(jnp.sum(mixed_rows, axis=1), "member")
    mixed_rows = (mixed_rows - product_sum[:, None] / ensemble) * spread_scale
    field = mixed_rows
    for step_index in range(NSTEP):
        spread = extended(diffusivity * field, (("state", 2),), 1)
        field = stencil_update(field, spread)
    return field


def solution(mesh):
    in_specs = (
        P("tm", "member", None, "state", None),
        P("tm", None, "state", None),
        P("state", None),
        P(),
    )
    out_specs = P("tm", "member", "state", None)
    return jax.shard_map(body, mesh=mesh, in_specs=in_specs, out_specs=out_specs, check_vma=False)
```

profile of v0, /device:TPU:0, one launch (start us, length us, event | category | flops | bytes accessed | tf_op | source)
XLA Modules:
  0.0 329.3 jit_solution(13562055111452354156)
XLA Ops:
  6.5 0.0 reduce-scatter.2.cloned.1.call-start
  6.5 8.4 %multiply_reduce_fusion = f32[16,48,1536,2]{2,1,0,3:T(8,128)S(1)} fusion(f32[16,48,1536,2]{2,1,0,3:T(8,128)} %bitcast.19, bf16[2,2,16,48,1536]{4,3,2,1,0:T(8,128)(2,1)} %param.4), kind=kLoop, calls=%fused_computation | loop fusion | flops 11796480 | bytes 28311552
  14.9 1.4 copy.14
  16.3 5.5 %copy.16 = f32[2,8,96,1536]{3,1,2,0:T(8,128)S(1)} copy(f32[2,8,96,1536]{3,2,1,0:T(8,128)S(1)} %bitcast.15) | data formatting | bytes 18874368
  21.8 17.1 %fusion.35 = f32[147456,16]{0,1:T(8,128)S(1)} fusion(f32[16,147456]{1,0:T(8,128)S(1)} %bitcast.13, f32[16,16]{1,0:T(8,128)S(1)} %copy-done), kind=kOutput, calls=%fused_computation.47 | convolution fusion | flops 452984832 | bytes 18875392 | tf_op jit(solution)/shard_map/dot_general | solution.py:43
  38.9 5.5 %copy.17 = f32[2,8,96,1536]{3,2,1,0:T(8,128)S(1)} copy(f32[2,8,96,1536]{3,1,2,0:T(8,128)S(1)} %bitcast.14) | data formatting | bytes 18874368
  44.4 9.3 %copy.5 = f32[16,2,48,1536]{3,0,2,1:T(8,128)} copy(f32[16,2,48,1536]{3,2,1,0:T(8,128)S(1)} %bitcast.16) | data formatting | bytes 18874368 | tf_op jit(solution)/shard_map/reshape | solution.py:47
  53.8 0.0 reduce-scatter.2.cloned.1.call-update
  53.8 0.0 copy-start.3
  53.8 0.0 all-reduce.2.cloned.1.call-start
  53.9 113.4 %reduce-scatter.2.cloned.1.call-done = f32[8,2,48,1536]{3,0,2,1:T(8,128)} async-done(((f32[16,2,48,1536]{3,0,2,1:T(8,128)}), f32[8,2,48,1536]{3,0,2,1:T(8,128)}) %reduce-scatter.2.cloned.1.call-update) | async-done | bytes 4718608 | tf_op jit(solution)/shard_map/reduce_scatter | solution.py:46
  167.3 4.4 %reduce_sum.9 = f32[8,48,1536]{2,0,1:T(8,128)} reduce(f32[8,2,48,1536]{3,0,2,1:T(8,128)} %reduce-scatter.2.cloned.1.call-done, f32[]{:T(128)} %constant.1.clone.1), dimensions={1}, to_apply=%region_1.0 | reduce | flops 589824 | bytes 7077892 | tf_op jit(solution)/shard_map/reduce_sum | solution.py:52
  171.7 0.0 all-reduce.2.cloned.1.call-update
  171.7 55.8 %all-reduce.2.cloned.1.call-done = f32[8,48,1536]{2,0,1:T(8,128)} async-done(((f32[8,48,1536]{2,0,1:T(8,128)}), f32[8,48,1536]{2,0,1:T(8,128)}) %all-reduce.2.cloned.1.call-update) | async-done | bytes 2359312 | tf_op jit(solution)/shard_map/psum | solution.py:52
  227.5 2.0 broadcast_multiply_fusion.3
  229.5 1.0 copy-done.2
  230.6 0.9 subtract_multiply_fusion
  231.5 5.4 %fusion.34 = (f32[8,2,48,1535]{3,0,2,1:T(8,128)}, f32[8,2,48,1535]{3,0,2,1:T(8,128)}) fusion(f32[8,2,48,1536]{3,0,2,1:T(8,128)S(1)} %subtract_multiply_fusion), kind=kLoop, calls=%fused_computation.46 | loop fusion | bytes 18862080 | tf_op jit(solution)/shard_map/jit(_roll_static)/slice | solution.py:28
  236.9 1.3 collective-permute-start
  238.2 4.6 %collective-permute-start.1 = (f32[8,2,1,1536]{3,0,2,1:T(8,128)S(1)}, f32[8,2,1,1536]{3,0,2,1:T(8,128)S(1)}, u32[]{:S(2)}, u32[]{:S(2)}) collective-permute-start(f32[8,2,1,1536]{3,0,2,1:T(8,128)S(1)} %get-tuple-element.30), channel_id=1, source_target_pairs={{0,1},{1,2},{2,3},{4,5},{5,6},{6,7},{8,9},{9,10},{10,11},{12,13},{... | collective-permute-start | bytes 294920 | tf_op jit(solution)/shard_map/ppermute | solution.py:16
  242.8 0.2 fusion.33
  242.9 0.5 collective-permute-done
  243.4 1.5 collective-permute-done.1
  244.9 0.6 copy-done.4
  245.6 8.9 %broadcast_multiply_fusion.2 = (f32[8,2,48,1536]{3,0,2,1:T(8,128)S(1)}, f32[8,2,48,1536]{3,0,2,1:T(8,128)}) fusion(f32[48,1536]{1,0:T(8,128)S(1)} %copy-done.3, f32[8,2,48,1536]{3,0,2,1:T(8,128)S(1)} %subtract_multiply_fusion, f32[8,2,48,1]{3,0,2,1:T(8,128)S(1)} %get-tuple-element.32, f32[8,2,48,1535]{3,0,2,1:T(8,128)} %get-tuple-element.34, ...), kind=kLoop, calls=%fused_computation.32 | loop fusion | flops 15335424 | bytes 31162368 | tf_op jit(solution)/shard_map/mul | solution.py:56
  254.5 5.4 %fusion.31 = (f32[8,2,48,1535]{3,0,2,1:T(8,128)}, f32[8,2,48,1535]{3,0,2,1:T(8,128)}) fusion(f32[8,2,48,1536]{3,0,2,1:T(8,128)S(1)} %get-tuple-element.9), kind=kLoop, calls=%fused_computation.43 | loop fusion | bytes 18862080 | tf_op jit(solution)/shard_map/jit(_roll_static)/slice | solution.py:28
  259.9 1.3 collective-permute-start.2
  261.2 4.9 %collective-permute-start.3 = (f32[8,2,1,1536]{3,0,2,1:T(8,128)S(1)}, f32[8,2,1,1536]{3,0,2,1:T(8,128)S(1)}, u32[]{:S(2)}, u32[]{:S(2)}) collective-permute-start(f32[8,2,1,1536]{3,0,2,1:T(8,128)S(1)} %get-tuple-element.24), channel_id=1, source_target_pairs={{0,1},{1,2},{2,3},{4,5},{5,6},{6,7},{8,9},{9,10},{10,11},{12,13},{... | collective-permute-start | bytes 294920 | tf_op jit(solution)/shard_map/ppermute | solution.py:16
  266.2 0.2 fusion.30
  266.4 0.5 collective-permute-done.2
  266.8 1.5 collective-permute-done.3
  268.4 8.8 %broadcast_multiply_fusion.1 = (f32[8,2,48,1536]{3,0,2,1:T(8,128)S(1)}, f32[8,2,48,1536]{3,0,2,1:T(8,128)}) fusion(f32[48,1536]{1,0:T(8,128)S(1)} %copy-done.3, f32[8,2,48,1536]{3,0,2,1:T(8,128)S(1)} %get-tuple-element.9, f32[8,2,48,1]{3,0,2,1:T(8,128)S(1)} %get-tuple-element.26, f32[8,2,48,1535]{3,0,2,1:T(8,128)} %get-tuple-element.28, ...), kind=kLoop, calls=%fused_computation.31 | loop fusion | flops 12976128 | bytes 28803072 | tf_op jit(solution)/shard_map/mul | solution.py:56
  277.2 5.4 %fusion.28 = (f32[8,2,48,1535]{3,0,2,1:T(8,128)}, f32[8,2,48,1535]{3,0,2,1:T(8,128)}) fusion(f32[8,2,48,1536]{3,0,2,1:T(8,128)S(1)} %get-tuple-element.7), kind=kLoop, calls=%fused_computation.40 | loop fusion | bytes 18862080 | tf_op jit(solution)/shard_map/jit(_roll_static)/slice | solution.py:28
  282.6 1.3 collective-permute-start.4
  283.9 4.9 %collective-permute-start.5 = (f32[8,2,1,1536]{3,0,2,1:T(8,128)S(1)}, f32[8,2,1,1536]{3,0,2,1:T(8,128)S(1)}, u32[]{:S(2)}, u32[]{:S(2)}) collective-permute-start(f32[8,2,1,1536]{3,0,2,1:T(8,128)S(1)} %get-tuple-element.18), channel_id=1, source_target_pairs={{0,1},{1,2},{2,3},{4,5},{5,6},{6,7},{8,9},{9,10},{10,11},{12,13},{... | collective-permute-start | bytes 294920 | tf_op jit(solution)/shard_map/ppermute | solution.py:16
  288.9 0.2 fusion.27
  289.1 0.5 collective-permute-done.4
  289.5 1.5 collective-permute-done.5
  291.1 8.4 %broadcast_multiply_fusion = (f32[8,2,48,1536]{3,0,2,1:T(8,128)S(1)}, f32[8,2,48,1536]{3,0,2,1:T(8,128)}) fusion(f32[48,1536]{1,0:T(8,128)S(1)} %copy-done.3, f32[8,2,48,1536]{3,0,2,1:T(8,128)S(1)} %get-tuple-element.7, f32[8,2,48,1]{3,0,2,1:T(8,128)S(1)} %get-tuple-element.20, f32[8,2,48,1535]{3,0,2,1:T(8,128)} %get-tuple-element.22, ...), kind=kLoop, calls=%fused_computation.30 | loop fusion | flops 12976128 | bytes 28803072 | tf_op jit(solution)/shard_map/mul | solution.py:56
  299.5 0.0 slice-start.1
  299.5 3.8 %fusion.23 = (f32[8,2,48,1535]{3,0,2,1:T(8,128)S(1)}, f32[8,2,48,1535]{3,0,2,1:T(8,128)}) fusion(f32[8,2,48,1536]{3,0,2,1:T(8,128)S(1)} %get-tuple-element.5), kind=kLoop, calls=%fused_computation.35 | loop fusion | bytes 18862080 | tf_op jit(solution)/shard_map/jit(_roll_static)/slice | solution.py:29
  303.4 1.3 collective-permute-start.6
  304.7 4.9 %collective-permute-start.7 = (f32[8,2,1,1536]{3,0,2,1:T(8,128)S(1)}, f32[8,2,1,1536]{3,0,2,1:T(8,128)S(1)}, u32[]{:S(2)}, u32[]{:S(2)}) collective-permute-start(f32[8,2,1,1536]{3,0,2,1:T(8,128)S(1)} %get-tuple-element.16), channel_id=1, source_target_pairs={{0,1},{1,2},{2,3},{4,5},{5,6},{6,7},{8,9},{9,10},{10,11},{12,13},{... | collective-permute-start | bytes 294920 | tf_op jit(solution)/shard_map/ppermute | solution.py:16
  309.6 0.2 fusion.24
  309.8 0.5 collective-permute-done.6
  310.3 1.5 collective-permute-done.7
  311.8 5.3 %fusion.3 = f32[8,2,48,1536]{3,0,2,1:T(8,128)S(1)} fusion(f32[8,2,48,1536]{3,0,2,1:T(8,128)S(1)} %get-tuple-element.5, f32[8,2,1,1536]{3,0,2,1:T(8,128)S(1)} %collective-permute-done.7, f32[8,2,48,1536]{3,0,2,1:T(8,128)S(1)} %bitcast.18, f32[8,2,1,1536]{3,0,2,1:T(8,128)S(1)} %collective-permute-done.6, f32[8,2,48,1535]{3,0,2,1:T(8,128)} %get-tuple-element.12, ...), kind=kLoop, calls=%fused_computation.5 | loop fusion | flops 11796480 | bytes 23789568 | tf_op jit(solution)/shard_map/sub | solution.py:25
  317.1 4.9 %copy.6 = f32[8,2,48,1536]{3,2,1,0:T(8,128)} copy(f32[8,2,48,1536]{3,0,2,1:T(8,128)S(1)} %fusion.3) | data formatting | bytes 9437184 | tf_op jit(solution)/shard_map/sub | solution.py:25
  (16 shorter events, 0.1 us)
Async XLA Ops:
  6.5 15.2 %copy-start = (f32[16,16]{1,0:T(8,128)S(1)}, f32[16,16]{1,0:T(8,128)}, u32[]{:S(2)}) copy-start(f32[16,16]{1,0:T(8,128)} %param.7) | copy-start | bytes 3076
  6.5 160.8 %reduce-scatter.2.cloned.1.call-start = ((), (), s32[]{:S(2)}) async-start(), calls=%async_computation.1 | async-start | bytes 14155776 | tf_op jit(solution)/shard_map/reduce_scatter | solution.py:46
  53.8 117.9 %copy-start.3 = (f32[48,1536]{1,0:T(8,128)S(1)}, f32[48,1536]{1,0:T(8,128)}, u32[]{:S(2)}) copy-start(f32[48,1536]{1,0:T(8,128)} %param.6) | copy-start | bytes 884740
  53.8 173.7 %all-reduce.2.cloned.1.call-start = ((), (), s32[]{:S(2)}) async-start(), calls=%async_computation.2 | async-start | bytes 4718592 | tf_op jit(solution)/shard_map/psum | solution.py:52
  227.5 3.0 copy-start.2
  236.9 6.5 %collective-permute-start = (f32[8,2,1,1536]{3,0,2,1:T(8,128)S(1)}, f32[8,2,1,1536]{3,0,2,1:T(8,128)S(1)}, u32[]{:S(2)}, u32[]{:S(2)}) collective-permute-start(f32[8,2,1,1536]{3,0,2,1:T(8,128)S(1)} %get-tuple-element.29), channel_id=1, source_target_pairs={{1,0},{2,1},{3,2},{5,4},{6,5},{7,6},{9,8},{10,9},{11,10},{13,12},{... | collective-permute-start | bytes 294920 | tf_op jit(solution)/shard_map/ppermute | solution.py:17
  238.2 6.8 %collective-permute-start.1 = (f32[8,2,1,1536]{3,0,2,1:T(8,128)S(1)}, f32[8,2,1,1536]{3,0,2,1:T(8,128)S(1)}, u32[]{:S(2)}, u32[]{:S(2)}) collective-permute-start(f32[8,2,1,1536]{3,0,2,1:T(8,128)S(1)} %get-tuple-element.30), channel_id=1, source_target_pairs={{0,1},{1,2},{2,3},{4,5},{5,6},{6,7},{8,9},{9,10},{10,11},{12,13},{... | collective-permute-start | bytes 294920 | tf_op jit(solution)/shard_map/ppermute | solution.py:16
  244.9 0.6 copy-start.4
  259.9 6.9 %collective-permute-start.2 = (f32[8,2,1,1536]{3,0,2,1:T(8,128)S(1)}, f32[8,2,1,1536]{3,0,2,1:T(8,128)S(1)}, u32[]{:S(2)}, u32[]{:S(2)}) collective-permute-start(f32[8,2,1,1536]{3,0,2,1:T(8,128)S(1)} %get-tuple-element.23), channel_id=1, source_target_pairs={{1,0},{2,1},{3,2},{5,4},{6,5},{7,6},{9,8},{10,9},{11,10},{13,12},{... | collective-permute-start | bytes 294920 | tf_op jit(solution)/shard_map/ppermute | solution.py:17
  261.2 7.1 %collective-permute-start.3 = (f32[8,2,1,1536]{3,0,2,1:T(8,128)S(1)}, f32[8,2,1,1536]{3,0,2,1:T(8,128)S(1)}, u32[]{:S(2)}, u32[]{:S(2)}) collective-permute-start(f32[8,2,1,1536]{3,0,2,1:T(8,128)S(1)} %get-tuple-element.24), channel_id=1, source_target_pairs={{0,1},{1,2},{2,3},{4,5},{5,6},{6,7},{8,9},{9,10},{10,11},{12,13},{... | collective-permute-start | bytes 294920 | tf_op jit(solution)/shard_map/ppermute | solution.py:16
  282.6 6.9 %collective-permute-start.4 = (f32[8,2,1,1536]{3,0,2,1:T(8,128)S(1)}, f32[8,2,1,1536]{3,0,2,1:T(8,128)S(1)}, u32[]{:S(2)}, u32[]{:S(2)}) collective-permute-start(f32[8,2,1,1536]{3,0,2,1:T(8,128)S(1)} %get-tuple-element.17), channel_id=1, source_target_pairs={{1,0},{2,1},{3,2},{5,4},{6,5},{7,6},{9,8},{10,9},{11,10},{13,12},{... | collective-permute-start | bytes 294920 | tf_op jit(solution)/shard_map/ppermute | solution.py:17
  283.9 7.1 %collective-permute-start.5 = (f32[8,2,1,1536]{3,0,2,1:T(8,128)S(1)}, f32[8,2,1,1536]{3,0,2,1:T(8,128)S(1)}, u32[]{:S(2)}, u32[]{:S(2)}) collective-permute-start(f32[8,2,1,1536]{3,0,2,1:T(8,128)S(1)} %get-tuple-element.18), channel_id=1, source_target_pairs={{0,1},{1,2},{2,3},{4,5},{5,6},{6,7},{8,9},{9,10},{10,11},{12,13},{... | collective-permute-start | bytes 294920 | tf_op jit(solution)/shard_map/ppermute | solution.py:16
  299.5 12.3 %slice-start = ((s8[4718592]{0:T(1024)(128)(4,1)}), s8[4194304]{0:T(1024)(128)(4,1)S(1)}, s32[]{:S(2)}) async-start(s8[4718592]{0:T(1024)(128)(4,1)} %bitcast.17), calls=%async_computation.3 | async-start | bytes 8388608
  299.5 12.3 %slice-start.1 = ((s8[4718592]{0:T(1024)(128)(4,1)}), s8[524288]{0:T(1024)(128)(4,1)S(1)}, s32[]{:S(2)}) async-start(s8[4718592]{0:T(1024)(128)(4,1)} %bitcast.17), calls=%async_computation.4 | async-start | bytes 1048576
  303.4 6.9 %collective-permute-start.6 = (f32[8,2,1,1536]{3,0,2,1:T(8,128)S(1)}, f32[8,2,1,1536]{3,0,2,1:T(8,128)S(1)}, u32[]{:S(2)}, u32[]{:S(2)}) collective-permute-start(f32[8,2,1,1536]{3,0,2,1:T(8,128)S(1)} %get-tuple-element.15), channel_id=1, source_target_pairs={{1,0},{2,1},{3,2},{5,4},{6,5},{7,6},{9,8},{10,9},{11,10},{13,12},{... | collective-permute-start | bytes 294920 | tf_op jit(solution)/shard_map/ppermute | solution.py:17
  304.7 7.1 %collective-permute-start.7 = (f32[8,2,1,1536]{3,0,2,1:T(8,128)S(1)}, f32[8,2,1,1536]{3,0,2,1:T(8,128)S(1)}, u32[]{:S(2)}, u32[]{:S(2)}) collective-permute-start(f32[8,2,1,1536]{3,0,2,1:T(8,128)S(1)} %get-tuple-element.16), channel_id=1, source_target_pairs={{0,1},{1,2},{2,3},{4,5},{5,6},{6,7},{8,9},{9,10},{10,11},{12,13},{... | collective-permute-start | bytes 294920 | tf_op jit(solution)/shard_map/ppermute | solution.py:16
  311.8 10.2 %copy-start.1 = (f32[16,16]{1,0:T(8,128)S(1)}, f32[16,16]{1,0:T(8,128)}, u32[]{:S(2)}) copy-start(f32[16,16]{1,0:T(8,128)} %param.7) | copy-start | bytes 3076
Sparse Core Ops, SparseCore 0:
  53.9 113.3 reduce-scatter.1
  171.8 55.6 all-reduce.1
where the time goes:
time: 335 us; the launch traced here: 329 us
  waiting for transfers between devices  177 us (53%)
  local copies, waits for them, and re-layouts  49.2 us (15%)
  other arithmetic  47.1 us (14%)
  starting transfers between devices  24.5 us (7%)
  matrix products  17.1 us (5%)
  between operations  14 us (4%)
    reduce_scatter x1, waiting for transfers between devices, body(): lax.psum_scatter(product.reshape((lax.axis_size('tm') * local_levels,) +...  113 us
    psum x1, waiting for transfers between devices, body(): product_sum = lax.psum(jnp.sum(mixed_rows, axis=1), 'member')  55.8 us
    mul x5, other arithmetic, body(): spread = extended(diffusivity * field, (('state', 2),), 1)  27.1 us
    ppermute x4, starting transfers between devices, extended(): before = lax.ppermute(last, axis, up)  19.4 us
    dot_general x1, matrix products, body(): jnp.dot(vertical.T, flattened, precision=lax.Precision.HIGHEST, preferred...  17.1 us
    slice x6, local copies, waits for them, and re-layouts, stencil_update(): jnp.roll(middle, 1, -1)  16.9 us
    unnamed x16, local copies, waits for them, and re-layouts  12.6 us
    reshape x1, local copies, waits for them, and re-layouts, body(): product.reshape((lax.axis_size('tm') * local_levels,) + partial_value.sha...  9.35 us
  transfers between devices with their start and end apart: 10, of which 10 were waited for; matrix products, arithmetic and copies ran while one was open for 0% of the time, Pallas kernels for 0%

commit v1 on v0

v1 whole, which is shorter than its diff:
```python
import functools

import jax
import jax.numpy as jnp
from jax import lax
from jax.experimental import pallas as pl
from jax.experimental.pallas import tpu as pltpu
from jax.sharding import PartitionSpec as P

NSTEP = 4
HALO = 8
CHUNK = 16
VMEM_BYTES = 64 * 1000 * 1000


def kernel(
    tm_size, member_size, state_size, scale,
    members_ref, grad_ref, diff_ref, vertical_ref, out_ref,
    mem_v, grad_v, part, send, recv, field, local_sum, total, rs_buf, edges,
    diff_v, fbuf, va, vb,
    in_sem, diff_sem, xs_sem, xr_sem, rss_sem, rsr_sem, ags_sem, agr_sem,
    hs_sem, hr_sem, ds_sem, dr_sem, out_sem,
):
    slots, local, levels, rows, cols = mem_v.shape
    out_levels = field.shape[0]
    ensemble = local * member_size
    width = cols // member_size
    tm = lax.axis_index("tm")
    mine = lax.axis_index("member")
    state = lax.axis_index("state")
    has_up, has_down = state > 0, state < state_size - 1
    chunks = rows // CHUNK

    def in_copies(c):
        at = pl.ds(c * CHUNK, CHUNK)
        return (
            pltpu.make_async_copy(
                members_ref.at[:, :, :, at, :], mem_v.at[:, :, :, at, :], in_sem.at[0, c]
            ),
            pltpu.make_async_copy(grad_ref.at[:, :, at, :], grad_v.at[:, :, at, :], in_sem.at[1, c]),
        )

    for c in range(chunks):
        for copy in in_copies(c):
            copy.start()
    diff_in = pltpu.make_async_copy(diff_ref, diff_v.at[pl.ds(HALO, rows), :], diff_sem)
    diff_in.start()

    barrier = pltpu.get_barrier_semaphore()
    for d in range(1, tm_size):
        pl.semaphore_signal(barrier, inc=1, device_id={"tm": lax.rem(tm + d, tm_size)})
    for d in range(1, member_size):
        pl.semaphore_signal(barrier, inc=1, device_id={"member": lax.rem(mine + d, member_size)})

    @pl.when(has_up)
    def _():
        pl.semaphore_signal(barrier, inc=1, device_id={"state": state - 1})

    @pl.when(has_down)
    def _():
        pl.semaphore_signal(barrier, inc=1, device_id={"state": state + 1})

    sides = has_up.astype(jnp.int32) + has_down.astype(jnp.int32)
    pl.semaphore_wait(barrier, tm_size + member_size - 2 + sides)

    def x_copy(d, lev, at):
        return pltpu.make_async_remote_copy(
            src_ref=send.at[d - 1, lev, :, at, :],
            dst_ref=recv.at[d - 1, lev, :, at, :],
            send_sem=xs_sem.at[d - 1, lev],
            recv_sem=xr_sem.at[d - 1, lev],
            device_id={"tm": lax.rem(tm + d, tm_size)},
        )

    def mix(source_level, dst, tile0, tiles):
        def one(i, carry):
            m = lax.rem(i, local)
            at = pl.ds(pl.multiple_of((tile0 + i // local) * 8, 8), 8)
            acc = vertical_ref[0, source_level] * part[0, m, at, :]
            for j in range(1, levels):
                acc = acc + vertical_ref[j, source_level] * part[j, m, at, :]
            dst[m, at, :] = acc
            return carry

        lax.fori_loop(0, tiles * local, one, 0)

    def send_level(d, lev):
        return lax.rem(tm + d, tm_size) * out_levels + lev

    for c in range(chunks):
        at = pl.ds(c * CHUNK, CHUNK)
        for copy in in_copies(c):
            copy.wait()

        def slot_sum(j, carry):
            for m in range(local):
                acc = mem_v[0, m, j, at, :].astype(jnp.float32) * grad_v[0, j, at, :]
                for s in range(1, slots):
                    acc = acc + mem_v[s, m, j, at, :].astype(jnp.float32) * grad_v[s, j, at, :]
                part[j, m, at, :] = acc
            return carry

        lax.fori_loop(0, levels, slot_sum, 0)
        for d in range(1, tm_size):
            mix(send_level(d, 0), send.at[d - 1, 0], c * (CHUNK // 8), CHUNK // 8)
            x_copy(d, 0, at).start()

    full = pl.ds(0, rows)

    def send_rest(lev, carry):
        for d in range(1, tm_size):
            mix(send_level(d, lev), send.at[d - 1, lev], 0, rows // 8)
            x_copy(d, lev, full).start()
        return carry

    lax.fori_loop(1, out_levels, send_rest, 0)

    diff_in.wait()

    def neighbour_copy(up, src, dst, send_sem, recv_sem):
        return pltpu.make_async_remote_copy(
            src_ref=src,
            dst_ref=dst,
            send_sem=send_sem,
            recv_sem=recv_sem,
            device_id={"state": state - 1 if up else state + 1},
        )

    def diff_copy(up):
        src = HALO if up else rows
        dst = rows + HALO if up else 0
        k = 1 if up else 0
        return neighbour_copy(
            up, diff_v.at[pl.ds(src, HALO), :], diff_v.at[pl.ds(dst, HALO), :], ds_sem.at[k], dr_sem.at[k]
        )

    def edge_copy(up, lev):
        src = 0 if up else rows - HALO
        k = 1 if up else 0
        return neighbour_copy(
            up, field.at[lev, :, pl.ds(src, HALO), :], edges.at[lev, k], hs_sem.at[k, lev], hr_sem.at[k, lev]
        )

    @pl.when(has_up)
    def _():
        diff_copy(True).start()

    @pl.when(has_down)
    def _():
        diff_copy(False).start()

    def clear_edges(k):
        diff_v[pl.ds(k * (rows + HALO), HALO), :] = jnp.zeros((HALO, cols), jnp.float32)

        def one(lev, carry):
            edges[lev, k] = jnp.zeros(edges.shape[2:], jnp.float32)
            return carry

        lax.fori_loop(0, out_levels, one, 0)

    @pl.when(jnp.logical_not(has_up))
    def _():
        clear_edges(0)

    @pl.when(jnp.logical_not(has_down))
    def _():
        clear_edges(1)

    for v in (va, vb):
        for m in range(local):
            v[m, pl.ds(0, 8), :] = jnp.zeros((8, cols), jnp.float32)
            v[m, pl.ds(rows + 2 * HALO + 8, 8), :] = jnp.zeros((8, cols), jnp.float32)

    def own(lev, carry):
        mix(tm * out_levels + lev, field.at[lev], 0, rows // 8)
        return carry

    lax.fori_loop(0, out_levels, own, 0)

    @pl.when(has_up)
    def _():
        diff_copy(True).wait_send()
        diff_copy(False).wait_recv()

    @pl.when(has_down)
    def _():
        diff_copy(False).wait_send()
        diff_copy(True).wait_recv()

    def lane_slice(owner):
        return pl.ds(pl.multiple_of(owner * width, 128), width)

    def rs_copy(d, lev):
        peer = lax.rem(mine + d, member_size)
        return pltpu.make_async_remote_copy(
            src_ref=local_sum.at[lev, :, lane_slice(peer)],
            dst_ref=rs_buf.at[lev, d - 1],
            send_sem=rss_sem.at[d - 1, lev],
            recv_sem=rsr_sem.at[d - 1, lev],
            device_id={"member": peer},
        )

    def ag_copy(d, lev, owner):
        return pltpu.make_async_remote_copy(
            src_ref=total.at[lev, :, lane_slice(owner)],
            dst_ref=total.at[lev, :, lane_slice(owner)],
            send_sem=ags_sem.at[d - 1, lev],
            recv_sem=agr_sem.at[d - 1, lev],
            device_id={"member": lax.rem(mine + d, member_size)},
        )

    def arrive(lev):
        for d in range(1, tm_size):
            x_copy(d, lev, full).wait_recv()

        def one(i, carry):
            at = pl.ds(pl.multiple_of(i * 8, 8), 8)
            acc = None
            for m in range(local):
                value = field[lev, m, at, :]
                for d in range(1, tm_size):
                    value = value + recv[d - 1, lev, m, at, :]
                field[lev, m, at, :] = value
                acc = value if acc is None else acc + value
            local_sum[lev, at, :] = acc
            return carry

        lax.fori_loop(0, rows // 8, one, 0)
        for d in range(1, member_size):
            rs_copy(d, lev).start()

    def reduce(lev):
        for d in range(1, member_size):
            rs_copy(d, lev).wait_recv()
        at = lane_slice(mine)
        acc = local_sum[lev, :, at]
        for d in range(1, member_size):
            acc = acc + rs_buf[lev, d - 1]
        total[lev, :, at] = acc * (1.0 / ensemble)
        for d in range(1, member_size):
            ag_copy(d, lev, mine).start()

    def centre(lev):
        for d in range(1, member_size):
            ag_copy(d, lev, lax.rem(mine + member_size - d, member_size)).wait_recv()

        def one(i, carry):
            at = pl.ds(pl.multiple_of(i * 8, 8), 8)
            mean = total[lev, at, :]
            for m in range(local):
                field[lev, m, at, :] = (field[lev, m, at, :] - mean) * scale
            return carry

        lax.fori_loop(0, rows // 8, one, 0)

        @pl.when(has_up)
        def _():
            edge_copy(True, lev).start()

        @pl.when(has_down)
        def _():
            edge_copy(False, lev).start()

    tiles = (rows + 2 * HALO) // 8

    def filter_level(lev):
        @pl.when(has_up)
        def _():
            edge_copy(True, lev).wait_send()
            edge_copy(False, lev).wait_recv()

        @pl.when(has_down)
        def _():
            edge_copy(False, lev).wait_send()
            edge_copy(True, lev).wait_recv()

        def one(m, carry):
            for i in range(tiles):
                if i == 0:
                    value = edges[lev, 0, m]
                elif i == tiles - 1:
                    value = edges[lev, 1, m]
                else:
                    value = field[lev, m, pl.ds(8 * (i - 1), 8), :]
                fbuf[m, pl.ds(8 * i, 8), :] = value
                va[m, pl.ds(8 * i + 8, 8), :] = value * diff_v[pl.ds(8 * i, 8), :]
            now, later = va, vb
            for step in range(NSTEP):
                last = step == NSTEP - 1
                for i in range(1 if last else 0, tiles - 1 if last else tiles):
                    mid = now[m, pl.ds(8 * i + 8, 8), :]
                    value = (
                        fbuf[m, pl.ds(8 * i, 8), :]
                        + now[m, pl.ds(8 * i + 9, 8), :]
                        + now[m, pl.ds(8 * i + 7, 8), :]
                        + pltpu.roll(mid, 1, 1)
                        + pltpu.roll(mid, cols - 1, 1)
                        - 4.0 * mid
                    )
                    if last:
                        field[lev, m, pl.ds(8 * (i - 1), 8), :] = value
                    else:
                        fbuf[m, pl.ds(8 * i, 8), :] = value
                        later[m, pl.ds(8 * i + 8, 8), :] = value * diff_v[pl.ds(8 * i, 8), :]
                now, later = later, now
            return carry

        lax.fori_loop(0, local, one, 0)
        out_copy(lev).start()

    def out_copy(lev):
        return pltpu.make_async_copy(field.at[lev], out_ref.at[lev], out_sem.at[lev])

    arrive(0)
    reduce(0)

    def step(lev, carry):
        arrive(lev)
        centre(lev - 1)
        reduce(lev)
        filter_level(lev - 1)
        return carry

    lax.fori_loop(1, out_levels, step, 0)
    centre(out_levels - 1)
    filter_level(out_levels - 1)

    def finish(lev, carry):
        for d in range(1, tm_size):
            x_copy(d, lev, full).wait_send()
        for d in range(1, member_size):
            rs_copy(d, lev).wait_send()
            ag_copy(d, lev, mine).wait_send()
        out_copy(lev).wait()
        return carry

    lax.fori_loop(0, out_levels, finish, 0)


def solution(mesh):
    tm_size, member_size, state_size = (mesh.shape[a] for a in ("tm", "member", "state"))

    def body(members, slot_grad, diffusivity, vertical):
        slots, local, levels, rows, cols = members.shape
        out_levels = levels // tm_size
        width = cols // member_size
        f32 = jnp.float32
        dma = pltpu.SemaphoreType.DMA
        chunks = rows // CHUNK
        scale = float(local * member_size - 1) ** -0.5
        block = (out_levels, local, rows, cols)
        padded = (local, rows + 2 * HALO + 16, cols)
        scratch = [
            pltpu.VMEM(members.shape, members.dtype),
            pltpu.VMEM(slot_grad.shape, f32),
            pltpu.VMEM((levels, local, rows, cols), f32),
            pltpu.VMEM((tm_size - 1,) + block, f32),
            pltpu.VMEM((tm_size - 1,) + block, f32),
            pltpu.VMEM(block, f32),
            pltpu.VMEM((out_levels, rows, cols), f32),
            pltpu.VMEM((out_levels, rows, cols), f32),
            pltpu.VMEM((out_levels, member_size - 1, rows, width), f32),
            pltpu.VMEM((out_levels, 2, local, HALO, cols), f32),
            pltpu.VMEM((rows + 2 * HALO, cols), f32),
            pltpu.VMEM((local, rows + 2 * HALO, cols), f32),
            pltpu.VMEM(padded, f32),
            pltpu.VMEM(padded, f32),
            dma((2, chunks)),
            dma,
            dma((tm_size - 1, out_levels)),
            dma((tm_size - 1, out_levels)),
            dma((member_size - 1, out_levels)),
            dma((member_size - 1, out_levels)),
            dma((member_size - 1, out_levels)),
            dma((member_size - 1, out_levels)),
            dma((2, out_levels)),
            dma((2, out_levels)),
            dma((2,)),
            dma((2,)),
            dma((out_levels,)),
        ]
        hbm = pl.BlockSpec(memory_space=pl.ANY)
        return pl.pallas_call(
            functools.partial(kernel, tm_size, member_size, state_size, scale),
            out_shape=jax.ShapeDtypeStruct(block, f32),
            in_specs=[hbm, hbm, hbm, pl.BlockSpec(memory_space=pltpu.SMEM)],
            out_specs=hbm,
            scratch_shapes=scratch,
            compiler_params=pltpu.CompilerParams(
                collective_id=0, has_side_effects=True, vmem_limit_bytes=VMEM_BYTES
            ),
        )(members, slot_grad, diffusivity, vertical)

    in_specs = (
        P("tm", "member", None, "state", None),
        P("tm", None, "state", None),
        P("state", None),
        P(),
    )
    out_specs = P("tm", "member", "state", None)
    return jax.shard_map(body, mesh=mesh, in_specs=in_specs, out_specs=out_specs, check_vma=False)
```

time: 335 us -> 131 us (0.39); the launches traced: 329 us -> 131 us
  waiting for transfers between devices: 177 us -> 0 us
  Pallas kernels: 0 us -> 126 us
  other arithmetic: 47.1 us -> 0 us
  local copies, waits for them, and re-layouts: 49.2 us -> 4.96 us
  starting transfers between devices: 24.5 us -> 0 us
  matrix products: 17.1 us -> 0 us
  between operations: 14 us -> 0.01 us
    pallas_call x0 -> x1, Pallas kernels: none -> 126 us  [body(): pl.pallas_call(functools.partial(kernel, tm_size, member_size, state_size...]
    reduce_scatter x1 -> x0, waiting for transfers between devices: 113 us -> none  [body(): lax.psum_scatter(product.reshape((lax.axis_size('tm') * local_levels,) +...]
    psum x1 -> x0, waiting for transfers between devices: 55.8 us -> none  [body(): product_sum = lax.psum(jnp.sum(mixed_rows, axis=1), 'member')]
    mul x5 -> x0, other arithmetic: 27.1 us -> none  [body(): spread = extended(diffusivity * field, (('state', 2),), 1)]
    ppermute x8 -> x0, starting transfers between devices: 24.5 us -> none  [the longest x4 19.4 us: extended(): before = lax.ppermute(last, axis, up)]
    slice x12 -> x0, local copies, waits for them, and re-layouts: 20.9 us -> none  [the longest x6 16.9 us: stencil_update(): jnp.roll(middle, 1, -1)]
    dot_general x1 -> x0, matrix products: 17.1 us -> none  [body(): jnp.dot(vertical.T, flattened, precision=lax.Precision.HIGHEST, preferred...]
    reshape x1 -> x0, local copies, waits for them, and re-layouts: 9.35 us -> none  [body(): product.reshape((lax.axis_size('tm') * local_levels,) + partial_value.sha...]
  transfers between devices with their start and end apart: 10 -> 0, of which waited for: 10 -> 0; matrix products, arithmetic and copies ran while one was open for 0% -> 0% of each run, Pallas kernels for 0% -> 0%
where the time goes in v1:
time: 131 us
  Pallas kernels  126 us (96%)
  local copies, waits for them, and re-layouts  4.96 us (4%)
    pallas_call x1, Pallas kernels, body(): pl.pallas_call(functools.partial(kernel, tm_size, member_size, state_size...  126 us
    unnamed x1, local copies, waits for them, and re-layouts  4.96 us

profile of v1, /device:TPU:0, one launch (start us, length us, event | category | flops | bytes accessed | tf_op | source)
XLA Modules:
  0.0 131.0 jit_solution(13423024703132059123)
XLA Ops:
  0.0 126.0 %shard_map.46 = f32[8,2,48,1536]{3,2,1,0:T(8,128)} custom-call(bf16[2,2,16,48,1536]{4,3,2,1,0:T(8,128)(2,1)} %members_ref.1, f32[2,16,48,1536]{3,2,1,0:T(8,128)} %grad_ref.1, f32[48,1536]{1,0:T(8,128)} %diff_ref.1, f32[16,16]{1,0:T(8,128)} %vertical_ref.1), custom_call_target="tpu_custom_call" | custom-call | tf_op jit(solution)/shard_map/pallas_call | solution.py:383
  126.0 5.0 %copy.6 = f32[8,2,48,1536]{3,2,1,0:T(8,128)} copy(f32[8,2,48,1536]{3,2,1,0:T(8,128)} %shard_map.46) | data formatting | bytes 9437184

commit v2 on v1

--- a/solution.py
+++ b/solution.py
@@ -16,9 +16,9 @@
 def kernel(
     tm_size, member_size, state_size, scale,
     members_ref, grad_ref, diff_ref, vertical_ref, out_ref,
-    mem_v, grad_v, part, send, recv, field, local_sum, total, rs_buf, edges,
+    mem_v, grad_v, part, send, recv, gauge, field, local_sum, total, rs_buf, edges,
     diff_v, fbuf, va, vb,
-    in_sem, diff_sem, xs_sem, xr_sem, rss_sem, rsr_sem, ags_sem, agr_sem,
+    in_sem, diff_sem, xs_sem, xr_sem, gs_sem, gr_sem, rss_sem, rsr_sem, ags_sem, agr_sem,
     hs_sem, hr_sem, ds_sem, dr_sem, out_sem,
 ):
     slots, local, levels, rows, cols = mem_v.shape
@@ -63,26 +63,55 @@
     sides = has_up.astype(jnp.int32) + has_down.astype(jnp.int32)
     pl.semaphore_wait(barrier, tm_size + member_size - 2 + sides)
 
-    def x_copy(d, lev, at):
+    slots_x = local * member_size
+
+    def x_copy(d, lev, first, at):
+        which = pl.ds(first, slots_x - first)
         return pltpu.make_async_remote_copy(
-            src_ref=send.at[d - 1, lev, :, at, :],
-            dst_ref=recv.at[d - 1, lev, :, at, :],
+            src_ref=send.at[d - 1, lev, which, at, :],
+            dst_ref=recv.at[d - 1, lev, which, at, :],
             send_sem=xs_sem.at[d - 1, lev],
             recv_sem=xr_sem.at[d - 1, lev],
             device_id={"tm": lax.rem(tm + d, tm_size)},
         )
 
-    def mix(source_level, dst, tile0, tiles):
+    def gauge_copy(d, e, lev):
+        return pltpu.make_async_remote_copy(
+            src_ref=send.at[d - 1, lev, 0],
+            dst_ref=gauge.at[d - 1, lev, e - 1],
+            send_sem=gs_sem.at[d - 1, e - 1, lev],
+            recv_sem=gr_sem.at[d - 1, e - 1, lev],
+            device_id={"member": lax.rem(mine + e, member_size)},
+        )
+
+    def mix(source_level, store, tile0, tiles):
         def one(i, carry):
             m = lax.rem(i, local)
             at = pl.ds(pl.multiple_of((tile0 + i // local) * 8, 8), 8)
             acc = vertical_ref[0, source_level] * part[0, m, at, :]
             for j in range(1, levels):
                 acc = acc + vertical_ref[j, source_level] * part[j, m, at, :]
-            dst[m, at, :] = acc
+            store(m, at, acc)
             return carry
 
         lax.fori_loop(0, tiles * local, one, 0)
+
+    def places_before(owner):
+        return lax.rem(mine + member_size - owner, member_size)
+
+    def mix_send(d, lev, tile0, tiles):
+        def store(m, at, acc):
+            for owner in range(member_size):
+                slot = m * member_size + places_before(owner)
+                send[d - 1, lev, slot, at, :] = acc[:, owner * width : (owner + 1) * width]
+
+        mix(send_level(d, lev), store, tile0, tiles)
+
+    def mix_own(lev):
+        def store(m, at, acc):
+            field[lev, m, at, :] = acc
+
+        mix(tm * out_levels + lev, store, 0, rows // 8)
 
     def send_level(d, lev):
         return lax.rem(tm + d, tm_size) * out_levels + lev
@@ -102,18 +131,46 @@
 
         lax.fori_loop(0, levels, slot_sum, 0)
         for d in range(1, tm_size):
-            mix(send_level(d, 0), send.at[d - 1, 0], c * (CHUNK // 8), CHUNK // 8)
-            x_copy(d, 0, at).start()
+            mix_send(d, 0, c * (CHUNK // 8), CHUNK // 8)
+            x_copy(d, 0, 0, at).start()
 
     full = pl.ds(0, rows)
 
-    def send_rest(lev, carry):
+    def open_level(lev):
         for d in range(1, tm_size):
-            mix(send_level(d, lev), send.at[d - 1, lev], 0, rows // 8)
-            x_copy(d, lev, full).start()
+            mix_send(d, lev, 0, rows // 8)
+            for e in range(1, member_size):
+                gauge_copy(d, e, lev).start()
+            recv[d - 1, lev, 0] = jnp.zeros((rows, width), jnp.float32)
+
+    def send_rest(lev):
+        for d in range(1, tm_size):
+            for e in range(1, member_size):
+                gauge_copy(d, e, lev).wait_recv()
+
+            def one(i, carry):
+                at = pl.ds(pl.multiple_of(i * 8, 8), 8)
+                for e in range(member_size):
+                    common = send[d - 1, lev, 0, at, :] if e == 0 else gauge[d - 1, lev, e - 1, at, :]
+                    for m in range(1 if e == 0 else 0, local):
+                        slot = m * member_size + e
+                        send[d - 1, lev, slot, at, :] = send[d - 1, lev, slot, at, :] - common
+                return carry
+
+            lax.fori_loop(0, rows // 8, one, 0)
+            x_copy(d, lev, 1, full).start()
+
+    def ahead(lev, carry):
+        open_level(lev)
+        mix_own(lev)
+        send_rest(lev - 1)
         return carry
 
-    lax.fori_loop(1, out_levels, send_rest, 0)
+    open_level(1)
+    mix_own(0)
+    mix_own(1)
+    lax.fori_loop(2, out_levels, ahead, 0)
+    send_rest(out_levels - 1)
 
     diff_in.wait()
 
@@ -170,12 +227,6 @@
         for m in range(local):
             v[m, pl.ds(0, 8), :] = jnp.zeros((8, cols), jnp.float32)
             v[m, pl.ds(rows + 2 * HALO + 8, 8), :] = jnp.zeros((8, cols), jnp.float32)
-
-    def own(lev, carry):
-        mix(tm * out_levels + lev, field.at[lev], 0, rows // 8)
-        return carry
-
-    lax.fori_loop(0, out_levels, own, 0)
 
     @pl.when(has_up)
     def _():
@@ -209,20 +260,22 @@
             device_id={"member": lax.rem(mine + d, member_size)},
         )
 
-    def arrive(lev):
+    def arrive(lev, first):
         for d in range(1, tm_size):
-            x_copy(d, lev, full).wait_recv()
+            x_copy(d, lev, first, full).wait_recv()
 
         def one(i, carry):
             at = pl.ds(pl.multiple_of(i * 8, 8), 8)
-            acc = None
-            for m in range(local):
-                value = field[lev, m, at, :]
-                for d in range(1, tm_size):
-                    value = value + recv[d - 1, lev, m, at, :]
-                field[lev, m, at, :] = value
-                acc = value if acc is None else acc + value
-            local_sum[lev, at, :] = acc
+            for owner in range(member_size):
+                lanes = pl.ds(owner * width, width)
+                acc = None
+                for m in range(local):
+                    value = field[lev, m, at, lanes]
+                    for d in range(1, tm_size):
+                        value = value + recv[d - 1, lev, m * member_size + places_before(owner), at, :]
+                    field[lev, m, at, lanes] = value
+                    acc = value if acc is None else acc + value
+                local_sum[lev, at, lanes] = acc
             return carry
 
         lax.fori_loop(0, rows // 8, one, 0)
@@ -311,11 +364,11 @@
     def out_copy(lev):
         return pltpu.make_async_copy(field.at[lev], out_ref.at[lev], out_sem.at[lev])
 
-    arrive(0)
+    arrive(0, 0)
     reduce(0)
 
     def step(lev, carry):
-        arrive(lev)
+        arrive(lev, 1)
         centre(lev - 1)
         reduce(lev)
         filter_level(lev - 1)
@@ -325,16 +378,22 @@
     centre(out_levels - 1)
     filter_level(out_levels - 1)
 
-    def finish(lev, carry):
+    def finish(lev, first):
         for d in range(1, tm_size):
-            x_copy(d, lev, full).wait_send()
+            x_copy(d, lev, first, full).wait_send()
+            for e in range(1, member_size if first else 1):
+                gauge_copy(d, e, lev).wait_send()
         for d in range(1, member_size):
             rs_copy(d, lev).wait_send()
             ag_copy(d, lev, mine).wait_send()
         out_copy(lev).wait()
+
+    def finish_rest(lev, carry):
+        finish(lev, 1)
         return carry
 
-    lax.fori_loop(0, out_levels, finish, 0)
+    finish(0, 0)
+    lax.fori_loop(1, out_levels, finish_rest, 0)
 
 
 def solution(mesh):
@@ -354,8 +413,9 @@
             pltpu.VMEM(members.shape, members.dtype),
             pltpu.VMEM(slot_grad.shape, f32),
             pltpu.VMEM((levels, local, rows, cols), f32),
-            pltpu.VMEM((tm_size - 1,) + block, f32),
-            pltpu.VMEM((tm_size - 1,) + block, f32),
+            pltpu.VMEM((tm_size - 1, out_levels, local * member_size, rows, width), f32),
+            pltpu.VMEM((tm_size - 1, out_levels, local * member_size, rows, width), f32),
+            pltpu.VMEM((tm_size - 1, out_levels, member_size - 1, rows, width), f32),
             pltpu.VMEM(block, f32),
             pltpu.VMEM((out_levels, rows, cols), f32),
             pltpu.VMEM((out_levels, rows, cols), f32),
@@ -369,6 +429,8 @@
             dma,
             dma((tm_size - 1, out_levels)),
             dma((tm_size - 1, out_levels)),
+            dma((tm_size - 1, member_size - 1, out_levels)),
+            dma((tm_size - 1, member_size - 1, out_levels)),
             dma((member_size - 1, out_levels)),
             dma((member_size - 1, out_levels)),
             dma((member_size - 1, out_levels)),

time: 131 us -> 121 us (0.924)
  Pallas kernels: 126 us -> 115 us
    pallas_call x1, Pallas kernels: 126 us -> 115 us  [body(): pl.pallas_call(functools.partial(kernel, tm_size, member_size, state_size...]
where the time goes in v2:
time: 121 us; the launch traced here: 120 us
  Pallas kernels  115 us (95%)
  local copies, waits for them, and re-layouts  4.96 us (4%)
    pallas_call x1, Pallas kernels, body(): pl.pallas_call(functools.partial(kernel, tm_size, member_size, state_size...  115 us
    unnamed x1, local copies, waits for them, and re-layouts  4.96 us

profile of v2, /device:TPU:0, one launch (start us, length us, event | category | flops | bytes accessed | tf_op | source)
XLA Modules:
  0.0 120.4 jit_solution(9667319298576927233)
XLA Ops:
  0.0 115.4 %shard_map.46 = f32[8,2,48,1536]{3,2,1,0:T(8,128)} custom-call(bf16[2,2,16,48,1536]{4,3,2,1,0:T(8,128)(2,1)} %members_ref.1, f32[2,16,48,1536]{3,2,1,0:T(8,128)} %grad_ref.1, f32[48,1536]{1,0:T(8,128)} %diff_ref.1, f32[16,16]{1,0:T(8,128)} %vertical_ref.1), custom_call_target="tpu_custom_call" | custom-call | tf_op jit(solution)/shard_map/pallas_call | solution.py:445
  115.4 5.0 %copy.6 = f32[8,2,48,1536]{3,2,1,0:T(8,128)} copy(f32[8,2,48,1536]{3,2,1,0:T(8,128)} %shard_map.46) | data formatting | bytes 9437184
